TPU v7x, 32 devices: a whole 2x2x4 slice. The times are simulated.
32 devices in a mesh: row: 4 (over z), col: 8 (over y, x, core).
Axes of the slice: x: 2, y: 2, z: 4, core: 2. Of those that a mesh axis runs over, the one named last changes fastest.
Arguments:
- matrix: float32 [15360, 15360], P('row', 'col'), may hold values from -4 to 4
- rhs: float32 [15360, 4096], P('row', 'col'), may hold values from -6 to 6
- pivot_inverses: bfloat16 [2, 512, 512], replicated, may hold values from -0.046875 to 0.046875
- panel_order: int32 [2], replicated, may hold values from 0 to 29, as said below
Outputs:
- factored: bfloat16 [15360, 15360], P('row', 'col')
- updated_rhs: float32 [15360, 4096], P('row', 'col')
- rhs_norms: float32 [4096], P('col')
Inputs may be any that keep to these rules, and one draw needn't show every extreme that they name: `panel_order`: two different panel indices, one of which is the last panel, 29.
All inputs are finite; a program needn't handle non-finite values.
Results may differ from a plain program's by a relative error of at most 0.001.
Values sent between devices are 32-bit elements; how exact they have to be, the bound alone decides.
No kernel may reach another device: no remote copies, remote signals or barrier semaphores. Data moves between devices by JAX's collectives and lax.ppermute only.
A program may use at most 192 MiB of HBM per device.

v0:
```python
import jax
import jax.numpy as jnp
from jax import lax
from jax.sharding import PartitionSpec as P

N = 15360
PW = 512


def product(first, second):
    return jnp.dot(
        first, second, precision=lax.Precision.HIGHEST, preferred_element_type=jnp.float32
    )


def cut_along(values, start, length, axis_dim):
    return lax.dynamic_slice_in_dim(values, start, length, axis_dim)


def refresh(sub_block, mult_rows, upper_rows, row_keep, col_keep, fresh_col, placed):
    updated = sub_block - row_keep[:, None] * product(mult_rows, upper_rows * col_keep[None, :])
    return jnp.where((row_keep[:, None] > 0) & (fresh_col[None, :] > 0), placed, updated)


def on_device(matrix, rhs, pivot_inverses, panel_order):
    row_count = lax.axis_size("row")
    col_count = lax.axis_size("col")
    block_size = PW // row_count
    group_count = col_count // row_count
    col_index = lax.axis_index("col")
    row_len, col_len = matrix.shape
    row_block_id = jnp.arange(row_len, dtype=jnp.int32) // block_size
    col_block_id = jnp.arange(col_len, dtype=jnp.int32) // block_size

    def column_hit(panel_id):
        is_owner = col_index // row_count == panel_id % group_count
        return (
            ((col_block_id == panel_id // group_count) & is_owner).astype(jnp.float32),
            is_owner,
        )

    def take_slices(current, right_sides, panel_id):
        start = panel_id * block_size
        return (
            cut_along(current, start, block_size, 0),
            cut_along(right_sides, start, block_size, 0),
            cut_along(current, panel_id // group_count * block_size, block_size, 1),
        )

    current = matrix
    right_sides = rhs
    row_piece, rhs_piece, column_slab = take_slices(current, right_sides, panel_order[0])
    for section in range(2):
        panel_id = panel_order[section]
        row_keep = jnp.ones((row_len,), jnp.float32)
        col_keep = jnp.ones((col_len,), jnp.float32)
        for earlier in range(section + 1):
            row_keep = row_keep * (row_block_id != panel_order[earlier]).astype(jnp.float32)
            hit, owner_flag = column_hit(panel_order[earlier])
            col_keep = col_keep * (1.0 - hit)
        fresh_col, keep_is_owner = column_hit(panel_order[section])
        row_keep, col_keep, fresh_col, is_owner = (row_keep, col_keep, fresh_col, keep_is_owner)
        upper_rows, rhs_rows = (
            lax.all_gather(row_piece, "row", axis=0, tiled=True),
            lax.all_gather(rhs_piece, "row", axis=0, tiled=True),
        )
        inverse = pivot_inverses[section].astype(jnp.float32)
        own_rows = cut_along(inverse, col_index % row_count * block_size, block_size, 0)
        partial_value = jnp.where(is_owner, product(column_slab, own_rows), 0.0)
        multipliers = lax.psum(partial_value, "col")
        own_mult = cut_along(multipliers, col_index % row_count * block_size, block_size, 1)
        placed = lax.dynamic_update_slice_in_dim(
            jnp.zeros_like(current), own_mult, panel_id // group_count * block_size, 1
        )
        current = refresh(current, multipliers, upper_rows, row_keep, col_keep, fresh_col, placed)
        right_sides = right_sides - row_keep[:, None] * product(multipliers, rhs_rows)
        if section == 0:
            row_piece, rhs_piece, column_slab = take_slices(current, right_sides, panel_order[1])
    totals = lax.psum(jnp.sum(right_sides * right_sides, axis=0), "row")
    rhs_norms = jnp.sqrt(totals / N + 1e-06)
    return (current.astype(jnp.bfloat16), right_sides, rhs_norms)


def solution(mesh):
    in_specs = (P("row", "col"), P("row", "col"), P(), P())
    out_specs = (P("row", "col"), P("row", "col"), P("col"))
    return jax.shard_map(
        on_device, mesh=mesh, in_specs=in_specs, out_specs=out_specs, check_vma=False
    )
```

profile of v0, /device:TPU:0, one launch (start us, length us, event | category | flops | bytes accessed | tf_op | source)
XLA Modules:
  0.0 484.3 jit_solution(17791880367086263619)
XLA Ops:
  8.0 0.0 all-gather.9.cloned.1.call-start
  8.0 1.4 fusion.28
  10.1 1.7 constant_dynamic-slice_fusion.3
  11.8 0.0 all-gather.9.cloned.1.call-update
  11.8 0.0 all-reduce.3.cloned.1.call-start
  14.5 1.3 fusion.27
  15.7 6.9 %convolution_select_fusion.1 = f32[3840,512]{1,0:T(8,128)} fusion(pred[]{:T(512)S(6)} %eq.59, f32[3840,1920]{1,0:T(8,128)} %param.4, s32[]{:T(128)S(6)} %select_n.140, bf16[1,512,512]{2,1,0:T(8,128)(2,1)S(1)} %get-tuple-element.4, s32[]{:T(128)S(6)} %select_n.142), kind=kOutput, calls=%fused_computation.6 | convolution fusion | flops 3021864960 | bytes 9961481 | tf_op jit(solution)/shard_map/dot_general | solution.py:11
  22.6 0.0 all-reduce.3.cloned.1.call-update
  22.7 0.0 all-gather.5.cloned.1.call-start
  22.7 2.3 constant_dynamic-slice_fusion.2
  25.0 0.0 all-gather.5.cloned.1.call-update
  25.0 0.0 all-gather.11.cloned.1.call-start
  28.5 0.7 broadcast_compare_fusion
  29.2 0.7 fusion.15
  29.9 12.8 %all-gather.9.cloned.1.call-done = f32[512,512]{1,0:T(8,128)} async-done(((f32[128,512]{1,0:T(8,128)}), f32[512,512]{1,0:T(8,128)}) %all-gather.9.cloned.1.call-update) | async-done | bytes 1048592 | tf_op jit(solution)/shard_map/all_gather | solution.py:65
  42.6 103.8 %all-reduce.3.cloned.1.call-done = f32[3840,512]{1,0:T(8,128)} async-done(((f32[3840,512]{1,0:T(8,128)}), f32[3840,512]{1,0:T(8,128)}) %all-reduce.3.cloned.1.call-update) | async-done | bytes 7864336 | tf_op jit(solution)/shard_map/psum | solution.py:70
  146.4 16.6 %multiply_subtract_fusion.1 = f32[3840,512]{1,0:T(8,128)S(1)} fusion(f32[3840,512]{1,0:T(8,128)} %param.5, f32[3840,512]{1,0:T(8,128)} %all-reduce.3.cloned.1.call-done, f32[512,512]{1,0:T(8,128)} %all-gather.9.cloned.1.call-done, f32[3840]{0:T(1024)S(1)} %fusion.15), kind=kOutput, calls=%fused_computation.4 | convolution fusion | flops 12083527680 | bytes 24656896 | tf_op jit(solution)/shard_map/dot_general | solution.py:11
  163.0 0.0 copy-start
  163.0 3.2 copy-done
  166.2 0.7 constant_dynamic-slice_fusion
  167.0 0.0 all-gather.11.cloned.1.call-update
  167.0 0.2 all-reduce.5.cloned.1.call-start
  167.2 11.9 %broadcast.286.clone = f32[3840,1920]{1,0:T(8,128)} broadcast(f32[]{:T(128)} %constant.140.clone.1), dimensions={} | broadcast | bytes 29491204 | tf_op jit(solution)/shard_map/broadcast.6
  179.1 3.1 dynamic-slice_dynamic-update-slice_fusion.1
  182.2 0.0 all-gather.5.cloned.1.call-done
  182.2 61.2 %subtract_select_fusion = f32[3840,1920]{1,0:T(8,128)} fusion(f32[3840,1920]{1,0:T(8,128)} %dynamic-slice_dynamic-update-slice_fusion.1, f32[3840,1920]{1,0:T(8,128)} %param.4, f32[3840,512]{1,0:T(8,128)} %all-reduce.3.cloned.1.call-done, f32[3840]{0:T(1024)S(1)} %fusion.15, pred[1920]{0:T(1024)(128)(4,1)S(1)} %convert_compare_fusion, ...), kind=kOutput, calls=%fused_computation.1 | convolution fusion | flops 45328957440 | bytes 100298880 | tf_op jit(solution)/shard_map/dot_general | solution.py:11
  243.4 6.9 %convolution_select_fusion = f32[3840,512]{1,0:T(8,128)} fusion(pred[]{:T(512)S(6)} %eq.56, f32[3840,1920]{1,0:T(8,128)} %subtract_select_fusion, s32[]{:T(128)S(6)} %select_n.146, bf16[1,512,512]{2,1,0:T(8,128)(2,1)S(1)} %get-tuple-element.3, s32[]{:T(128)S(6)} %select_n.142), kind=kOutput, calls=%fused_computation.5 | convolution fusion | flops 3021864960 | bytes 9961481 | tf_op jit(solution)/shard_map/dot_general | solution.py:11
  250.3 0.0 all-reduce.5.cloned.1.call-update
  250.3 0.3 all-gather.7.cloned.1.call-start
  250.6 2.2 constant_dynamic-slice_fusion.1
  252.8 0.0 all-gather.7.cloned.1.call-update
  252.9 1.3 broadcast_compare_fusion.1
  254.2 1.3 fusion.14
  255.6 0.0 all-gather.11.cloned.1.call-done
  255.6 115.9 %all-reduce.5.cloned.1.call-done = f32[3840,512]{1,0:T(8,128)} async-done(((f32[3840,512]{1,0:T(8,128)}), f32[3840,512]{1,0:T(8,128)}) %all-reduce.5.cloned.1.call-update) | async-done | bytes 7864336 | tf_op jit(solution)/shard_map/psum | solution.py:70
  371.5 17.8 %multiply_reduce_fusion = (f32[512]{0:T(512)S(1)}, f32[3840,512]{1,0:T(8,128)}) fusion(f32[3840,512]{1,0:T(8,128)} %copy-done, f32[3840,512]{1,0:T(8,128)} %all-reduce.5.cloned.1.call-done, f32[512,512]{1,0:T(8,128)} %all-gather.11.cloned.1.call-done, f32[3840]{0:T(1024)S(1)} %fusion.14), kind=kOutput, calls=%fused_computation.2 | convolution fusion | flops 12087459840 | bytes 24658944 | tf_op jit(solution)/shard_map/dot_general | solution.py:11
  389.2 11.7 %psum.23 = f32[512]{0:T(512)S(1)} all-reduce(f32[512]{0:T(512)S(1)} %get-tuple-element.7), channel_id=1, replica_groups=mesh['row'=4,'col'=8] {'row'}, use_global_device_ids=true, to_apply=%region_3.4 | all-reduce | flops 512 | bytes 4096 | tf_op jit(solution)/shard_map/psum | solution.py:79
  400.9 0.6 add_sqrt_fusion
  401.5 11.6 %broadcast.286 = f32[3840,1920]{1,0:T(8,128)} broadcast(f32[]{:T(128)} %constant.140.clone.1), dimensions={} | broadcast | bytes 29491204 | tf_op jit(solution)/shard_map/broadcast.6
  413.1 3.1 dynamic-slice_dynamic-update-slice_fusion
  416.2 0.0 all-gather.7.cloned.1.call-done
  416.2 60.9 %select_convert_fusion = bf16[3840,1920]{1,0:T(8,128)(2,1)} fusion(f32[3840,1920]{1,0:T(8,128)} %dynamic-slice_dynamic-update-slice_fusion, f32[3840,1920]{1,0:T(8,128)} %subtract_select_fusion, f32[3840,512]{1,0:T(8,128)} %all-reduce.5.cloned.1.call-done, f32[3840]{0:T(1024)S(1)} %fusion.14, pred[1920]{0:T(1024)(128)(4,1)S(1)} %convert_compare_fusion.1, ...), kind=kOutput, calls=%fused_computation | convolution fusion | flops 45328957440 | bytes 85553280 | tf_op jit(solution)/shard_map/dot_general | solution.py:11
  (4 shorter events, 0.0 us)
Async XLA Ops:
  8.0 34.6 %all-gather.9.cloned.1.call-start = ((), (), s32[]{:S(2)}) async-start(), calls=%async_computation.4 | async-start | bytes 1310720 | tf_op jit(solution)/shard_map/all_gather | solution.py:65
  11.8 134.6 %all-reduce.3.cloned.1.call-start = ((), (), s32[]{:S(2)}) async-start(), calls=%async_computation | async-start | bytes 15728640 | tf_op jit(solution)/shard_map/psum | solution.py:70
  22.7 159.5 %all-gather.5.cloned.1.call-start = ((), (), s32[]{:S(2)}) async-start(), calls=%async_computation.1 | async-start | bytes 4915200 | tf_op jit(solution)/shard_map/all_gather | solution.py:64
  25.0 230.5 %all-gather.11.cloned.1.call-start = ((), (), s32[]{:S(2)}) async-start(), calls=%async_computation.5 | async-start | bytes 1310720 | tf_op jit(solution)/shard_map/all_gather | solution.py:65
  163.0 3.2 copy-start
  167.0 204.5 %all-reduce.5.cloned.1.call-start = ((), (), s32[]{:S(2)}) async-start(), calls=%async_computation.2 | async-start | bytes 15728640 | tf_op jit(solution)/shard_map/psum | solution.py:70
  250.3 165.9 %all-gather.7.cloned.1.call-start = ((), (), s32[]{:S(2)}) async-start(), calls=%async_computation.3 | async-start | bytes 4915200 | tf_op jit(solution)/shard_map/all_gather | solution.py:64
Sparse Core Ops, SparseCore 0:
  11.9 30.6 all-gather.8
  44.2 75.7 all-gather.4
  167.1 28.0 all-gather.10
  253.0 76.5 all-gather.6
Sparse Core Ops, SparseCore 1:
  22.7 123.6 all-reduce.2
  250.4 121.0 all-reduce.4
where the time goes:
time: 485 us; the launch traced here: 484 us
  waiting for transfers between devices  233 us (48%)
  matrix products  170 us (35%)
  local copies, waits for them, and re-layouts  42.5 us (9%)
  between operations  22 us (5%)
  blocking collectives  11.7 us (2%)
    psum x2, waiting for transfers between devices, on_device(): multipliers = lax.psum(partial_value, 'col')  220 us
    dot_general x6, matrix products, product(): jnp.dot(first, second, precision=lax.Precision.HIGHEST, preferred_element...  170 us
    another operation x2, local copies, waits for them, and re-layouts  23.5 us
    all_gather x2, waiting for transfers between devices, on_device(): lax.all_gather(rhs_piece, 'row', axis=0, tiled=True)  12.8 us
    psum x1, blocking collectives, on_device(): totals = lax.psum(jnp.sum(right_sides * right_sides, axis=0), 'row')  11.7 us
  transfers between devices with their start and end apart: 6, of which 3 were waited for; matrix products, arithmetic and copies ran while one was open for 31% of the time, Pallas kernels for 0%

commit v1 on v0

--- a/solution.py
+++ b/solution.py
@@ -67,7 +67,11 @@
         inverse = pivot_inverses[section].astype(jnp.float32)
         own_rows = cut_along(inverse, col_index % row_count * block_size, block_size, 0)
         partial_value = jnp.where(is_owner, product(column_slab, own_rows), 0.0)
-        multipliers = lax.psum(partial_value, "col")
+        multipliers = partial_value
+        for hop in (1, 2, 4):
+            multipliers = multipliers + lax.ppermute(
+                multipliers, "col", [(dev, dev ^ hop) for dev in range(8)]
+            )
         own_mult = cut_along(multipliers, col_index % row_count * block_size, block_size, 1)
         placed = lax.dynamic_update_slice_in_dim(
             jnp.zeros_like(current), own_mult, panel_id // group_count * block_size, 1

time: 485 us -> 986 us (2.03)
  waiting for transfers between devices: 233 us -> 667 us
  other arithmetic: 4.61 us -> 61.6 us
    ppermute x0 -> x6, waiting for transfers between devices: none -> 667 us  [on_device(): lax.ppermute(multipliers, 'col', [(dev, dev ^ hop) for dev in range(8)])]
    psum x2 -> x0, waiting for transfers between devices: 220 us -> none  [on_device(): multipliers = lax.psum(partial_value, 'col')]
    add x0 -> x6, other arithmetic: none -> 57 us  [on_device(): multipliers + lax.ppermute(multipliers, 'col', [(dev, dev ^ hop) for dev...]
    all_gather x2, waiting for transfers between devices: 12.8 us -> 0.02 us  [on_device(): lax.all_gather(rhs_piece, 'row', axis=0, tiled=True)]
  transfers between devices with their start and end apart: 6 -> 10, of which waited for: 3 -> 6; matrix products, arithmetic and copies ran while one was open for 31% -> 11% of each run, Pallas kernels for 0% -> 0%
where the time goes in v1:
time: 986 us; the launch traced here: 979 us
  waiting for transfers between devices  667 us (68%)
  matrix products  166 us (17%)
  other arithmetic  61.6 us (6%)
  local copies, waits for them, and re-layouts  42.2 us (4%)
  between operations  20.9 us (2%)
  blocking collectives  12.1 us (1%)
    ppermute x6, waiting for transfers between devices, on_device(): lax.ppermute(multipliers, 'col', [(dev, dev ^ hop) for dev in range(8)])  667 us
    dot_general x6, matrix products, product(): jnp.dot(first, second, precision=lax.Precision.HIGHEST, preferred_element...  166 us
    add x6, other arithmetic, on_device(): multipliers + lax.ppermute(multipliers, 'col', [(dev, dev ^ hop) for dev...  57 us
    another operation x2, local copies, waits for them, and re-layouts  23.2 us
  transfers between devices with their start and end apart: 10, of which 6 were waited for; matrix products, arithmetic and copies ran while one was open for 11% of the time, Pallas kernels for 0%

profile of v1, /device:TPU:0, one launch (start us, length us, event | category | flops | bytes accessed | tf_op | source)
XLA Modules:
  0.0 979.1 jit_solution(10929267179223101930)
XLA Ops:
  7.2 0.0 all-gather.5.cloned.1.call-start
  7.2 1.4 fusion.28
  11.2 1.3 fusion.27
  12.6 4.8 convolution_select_fusion.1
  17.4 0.6 collective-permute-start
  17.9 12.2 %collective-permute-done = f32[3840,512]{1,0:T(8,128)} collective-permute-done((f32[3840,512]{1,0:T(8,128)S(1)}, f32[3840,512]{1,0:T(8,128)}, u32[]{:S(2)}, u32[]{:S(2)}) %collective-permute-start) | collective-permute-done | bytes 7864352 | tf_op jit(solution)/shard_map/ppermute | solution.py:72
  30.1 8.4 add.100
  38.5 2.8 collective-permute-start.1
  41.3 169.7 %collective-permute-done.1 = f32[3840,512]{1,0:T(8,128)S(1)} collective-permute-done((f32[3840,512]{1,0:T(8,128)}, f32[3840,512]{1,0:T(8,128)S(1)}, u32[]{:S(2)}, u32[]{:S(2)}) %collective-permute-start.1) | collective-permute-done | bytes 7864352 | tf_op jit(solution)/shard_map/ppermute | solution.py:72
  211.1 8.4 add.101
  219.5 1.8 collective-permute-start.2
  221.9 2.2 constant_dynamic-slice_fusion.2
  224.1 0.0 all-gather.5.cloned.1.call-update
  224.2 0.2 all-gather.9.cloned.1.call-start
  227.2 0.7 broadcast_compare_fusion
  227.9 0.7 fusion.15
  228.5 162.0 %collective-permute-done.2 = f32[3840,512]{1,0:T(8,128)} collective-permute-done((f32[3840,512]{1,0:T(8,128)}, f32[3840,512]{1,0:T(8,128)}, u32[]{:S(2)}, u32[]{:S(2)}) %collective-permute-start.2) | collective-permute-done | bytes 7864352 | tf_op jit(solution)/shard_map/ppermute | solution.py:72
  390.5 10.6 %add.102 = f32[3840,512]{1,0:T(8,128)} add(f32[3840,512]{1,0:T(8,128)} %add.101, f32[3840,512]{1,0:T(8,128)} %collective-permute-done.2) | non-fusion elementwise | flops 1966080 | bytes 23592960 | tf_op jit(solution)/shard_map/add | solution.py:72
  401.1 11.6 %broadcast.286.clone = f32[3840,1920]{1,0:T(8,128)} broadcast(f32[]{:T(128)} %constant.140.clone.1), dimensions={} | broadcast | bytes 29491204 | tf_op jit(solution)/shard_map/broadcast.6
  412.8 3.1 dynamic-slice_dynamic-update-slice_fusion.1
  415.9 0.0 all-gather.5.cloned.1.call-done
  415.9 61.1 %subtract_select_fusion = f32[3840,1920]{1,0:T(8,128)} fusion(f32[3840,1920]{1,0:T(8,128)} %dynamic-slice_dynamic-update-slice_fusion.1, f32[3840,1920]{1,0:T(8,128)} %param.4, f32[3840,512]{1,0:T(8,128)} %add.102, f32[3840]{0:T(1024)S(1)} %fusion.15, pred[1920]{0:T(1024)(128)(4,1)S(1)} %convert_compare_fusion, ...), kind=kOutput, calls=%fused_computation.1 | convolution fusion | flops 45328957440 | bytes 100298880 | tf_op jit(solution)/shard_map/dot_general | solution.py:11
  477.0 4.8 convolution_select_fusion
  481.8 0.1 collective-permute-start.3
  481.9 12.5 %collective-permute-done.3 = f32[3840,512]{1,0:T(8,128)} collective-permute-done((f32[3840,512]{1,0:T(8,128)S(1)}, f32[3840,512]{1,0:T(8,128)}, u32[]{:S(2)}, u32[]{:S(2)}) %collective-permute-start.3) | collective-permute-done | bytes 7864352 | tf_op jit(solution)/shard_map/ppermute | solution.py:72
  494.4 8.4 add.105
  502.8 1.5 collective-permute-start.4
  504.3 1.7 constant_dynamic-slice_fusion.3
  506.0 0.0 all-gather.9.cloned.1.call-update
  506.0 0.4 all-gather.11.cloned.1.call-start
  506.4 168.0 %collective-permute-done.4 = f32[3840,512]{1,0:T(8,128)} collective-permute-done((f32[3840,512]{1,0:T(8,128)}, f32[3840,512]{1,0:T(8,128)}, u32[]{:S(2)}, u32[]{:S(2)}) %collective-permute-start.4) | collective-permute-done | bytes 7864352 | tf_op jit(solution)/shard_map/ppermute | solution.py:72
  674.4 10.6 %add.106 = f32[3840,512]{1,0:T(8,128)} add(f32[3840,512]{1,0:T(8,128)} %add.105, f32[3840,512]{1,0:T(8,128)} %collective-permute-done.4) | non-fusion elementwise | flops 1966080 | bytes 23592960 | tf_op jit(solution)/shard_map/add | solution.py:72
  685.1 1.5 collective-permute-start.5
  687.2 0.0 all-gather.9.cloned.1.call-done
  687.3 16.6 %multiply_subtract_fusion.1 = f32[3840,512]{1,0:T(8,128)S(1)} fusion(f32[3840,512]{1,0:T(8,128)} %param.5, f32[3840,512]{1,0:T(8,128)} %add.102, f32[512,512]{1,0:T(8,128)} %all-gather.9.cloned.1.call-done, f32[3840]{0:T(1024)S(1)} %fusion.15), kind=kOutput, calls=%fused_computation.4 | convolution fusion | flops 12083527680 | bytes 24656896 | tf_op jit(solution)/shard_map/dot_general | solution.py:11
  703.9 0.0 copy-start
  703.9 3.2 copy-done
  707.1 0.7 constant_dynamic-slice_fusion
  707.8 0.0 all-gather.11.cloned.1.call-update
  707.9 0.0 all-gather.7.cloned.1.call-start
  707.9 2.2 constant_dynamic-slice_fusion.1
  710.1 0.0 all-gather.7.cloned.1.call-update
  710.2 1.3 broadcast_compare_fusion.1
  711.6 1.3 fusion.14
  712.9 142.9 %collective-permute-done.5 = f32[3840,512]{1,0:T(8,128)} collective-permute-done((f32[3840,512]{1,0:T(8,128)}, f32[3840,512]{1,0:T(8,128)}, u32[]{:S(2)}, u32[]{:S(2)}) %collective-permute-start.5) | collective-permute-done | bytes 7864352 | tf_op jit(solution)/shard_map/ppermute | solution.py:72
  855.8 10.5 %add.107 = f32[3840,512]{1,0:T(8,128)} add(f32[3840,512]{1,0:T(8,128)} %add.106, f32[3840,512]{1,0:T(8,128)} %collective-permute-done.5) | non-fusion elementwise | flops 1966080 | bytes 23592960 | tf_op jit(solution)/shard_map/add | solution.py:72
  866.3 0.0 all-gather.11.cloned.1.call-done
  866.3 17.8 %multiply_reduce_fusion = (f32[512]{0:T(512)S(1)}, f32[3840,512]{1,0:T(8,128)}) fusion(f32[3840,512]{1,0:T(8,128)} %copy-done, f32[3840,512]{1,0:T(8,128)} %add.107, f32[512,512]{1,0:T(8,128)} %all-gather.11.cloned.1.call-done, f32[3840]{0:T(1024)S(1)} %fusion.14), kind=kOutput, calls=%fused_computation.2 | convolution fusion | flops 12087459840 | bytes 24658944 | tf_op jit(solution)/shard_map/dot_general | solution.py:11
  884.0 12.1 %psum.7 = f32[512]{0:T(512)S(1)} all-reduce(f32[512]{0:T(512)S(1)} %get-tuple-element.7), channel_id=1, replica_groups=mesh['row'=4,'col'=8] {'row'}, use_global_device_ids=true, to_apply=%region_1.2 | all-reduce | flops 512 | bytes 4096 | tf_op jit(solution)/shard_map/psum | solution.py:83
  896.1 0.6 add_sqrt_fusion
  896.7 11.6 %broadcast.286 = f32[3840,1920]{1,0:T(8,128)} broadcast(f32[]{:T(128)} %constant.140.clone.1), dimensions={} | broadcast | bytes 29491204 | tf_op jit(solution)/shard_map/broadcast.6
  908.3 3.1 dynamic-slice_dynamic-update-slice_fusion
  911.4 0.0 all-gather.7.cloned.1.call-done
  911.4 60.9 %select_convert_fusion = bf16[3840,1920]{1,0:T(8,128)(2,1)} fusion(f32[3840,1920]{1,0:T(8,128)} %dynamic-slice_dynamic-update-slice_fusion, f32[3840,1920]{1,0:T(8,128)} %subtract_select_fusion, f32[3840,512]{1,0:T(8,128)} %add.107, f32[3840]{0:T(1024)S(1)} %fusion.14, pred[1920]{0:T(1024)(128)(4,1)S(1)} %convert_compare_fusion.1, ...), kind=kOutput, calls=%fused_computation | convolution fusion | flops 45328957440 | bytes 85553280 | tf_op jit(solution)/shard_map/dot_general | solution.py:11
  (4 shorter events, 0.0 us)
Async XLA Ops:
  7.2 408.7 %all-gather.5.cloned.1.call-start = ((), (), s32[]{:S(2)}) async-start(), calls=%async_computation | async-start | bytes 4915200 | tf_op jit(solution)/shard_map/all_gather | solution.py:64
  17.4 12.7 %collective-permute-start = (f32[3840,512]{1,0:T(8,128)S(1)}, f32[3840,512]{1,0:T(8,128)}, u32[]{:S(2)}, u32[]{:S(2)}) collective-permute-start(f32[3840,512]{1,0:T(8,128)S(1)} %convolution_select_fusion.1), channel_id=1, source_target_pairs={{0,1},{1,0},{2,3},{3,2},{4,5},{5,4},{6,7},{7,6},{8,9},{9,8},{10,11... | collective-permute-start | bytes 23592968 | tf_op jit(solution)/shard_map/ppermute | solution.py:72
  38.5 172.6 %collective-permute-start.1 = (f32[3840,512]{1,0:T(8,128)}, f32[3840,512]{1,0:T(8,128)S(1)}, u32[]{:S(2)}, u32[]{:S(2)}) collective-permute-start(f32[3840,512]{1,0:T(8,128)} %add.100), channel_id=1, source_target_pairs={{0,2},{1,3},{2,0},{3,1},{4,6},{5,7},{6,4},{7,5},{8,10},{9,11},{10,... | collective-permute-start | bytes 23592968 | tf_op jit(solution)/shard_map/ppermute | solution.py:72
  219.5 171.0 %collective-permute-start.2 = (f32[3840,512]{1,0:T(8,128)}, f32[3840,512]{1,0:T(8,128)}, u32[]{:S(2)}, u32[]{:S(2)}) collective-permute-start(f32[3840,512]{1,0:T(8,128)} %add.101), channel_id=1, source_target_pairs={{0,4},{1,5},{2,6},{3,7},{4,0},{5,1},{6,2},{7,3},{8,12},{9,13},{10,... | collective-permute-start | bytes 23592968 | tf_op jit(solution)/shard_map/ppermute | solution.py:72
  224.2 463.1 %all-gather.9.cloned.1.call-start = ((), (), s32[]{:S(2)}) async-start(), calls=%async_computation.2 | async-start | bytes 1310720 | tf_op jit(solution)/shard_map/all_gather | solution.py:65
  481.8 12.6 %collective-permute-start.3 = (f32[3840,512]{1,0:T(8,128)S(1)}, f32[3840,512]{1,0:T(8,128)}, u32[]{:S(2)}, u32[]{:S(2)}) collective-permute-start(f32[3840,512]{1,0:T(8,128)S(1)} %convolution_select_fusion), channel_id=1, source_target_pairs={{0,1},{1,0},{2,3},{3,2},{4,5},{5,4},{6,7},{7,6},{8,9},{9,8},{10,11... | collective-permute-start | bytes 23592968 | tf_op jit(solution)/shard_map/ppermute | solution.py:72
  502.8 171.6 %collective-permute-start.4 = (f32[3840,512]{1,0:T(8,128)}, f32[3840,512]{1,0:T(8,128)}, u32[]{:S(2)}, u32[]{:S(2)}) collective-permute-start(f32[3840,512]{1,0:T(8,128)} %add.105), channel_id=1, source_target_pairs={{0,2},{1,3},{2,0},{3,1},{4,6},{5,7},{6,4},{7,5},{8,10},{9,11},{10,... | collective-permute-start | bytes 23592968 | tf_op jit(solution)/shard_map/ppermute | solution.py:72
  506.0 360.3 %all-gather.11.cloned.1.call-start = ((), (), s32[]{:S(2)}) async-start(), calls=%async_computation.3 | async-start | bytes 1310720 | tf_op jit(solution)/shard_map/all_gather | solution.py:65
  685.1 170.7 %collective-permute-start.5 = (f32[3840,512]{1,0:T(8,128)}, f32[3840,512]{1,0:T(8,128)}, u32[]{:S(2)}, u32[]{:S(2)}) collective-permute-start(f32[3840,512]{1,0:T(8,128)} %add.106), channel_id=1, source_target_pairs={{0,4},{1,5},{2,6},{3,7},{4,0},{5,1},{6,2},{7,3},{8,12},{9,13},{10,... | collective-permute-start | bytes 23592968 | tf_op jit(solution)/shard_map/ppermute | solution.py:72
  703.9 3.2 copy-start
  707.9 203.6 %all-gather.7.cloned.1.call-start = ((), (), s32[]{:S(2)}) async-start(), calls=%async_computation.1 | async-start | bytes 4915200 | tf_op jit(solution)/shard_map/all_gather | solution.py:64
Sparse Core Ops, SparseCore 0:
  224.3 76.6 all-gather.4
  506.1 28.2 all-gather.8
  708.0 28.2 all-gather.10
  737.7 75.7 all-gather.6
